TPU v7x, 32 devices: a whole 2x2x4 slice. The times are simulated.
32 devices in a mesh: slab: 4 (over y, x), sta: 8 (over z, core).
Axes of the slice: x: 2, y: 2, z: 4, core: 2. Of those that a mesh axis runs over, the one named last changes fastest.
Arguments:
- station_place: float32 [32, 2], P('sta'), may hold values from 0 to 1
- station_height: float32 [32], P('sta'), may hold values from 2 to 8
- cell_weight: float32 [256, 256, 64], P('slab'), may hold values from 0.5 to 2
- kept: int32 [4, 32, 16], P('slab', 'sta'), may hold values from 0 to 8191, as said below
- dest: int32 [4, 32, 16, 1], P('slab', 'sta'), may hold values from 0 to 7; in each aligned block of 64 rows (0 to 63, 64 to 127, ..., all dimensions but the last counted through in order) at most 24 rows name the same one
Outputs:
- owned_blocks: float32 [4, 8, 8, 24, 128], P('slab', 'sta')
Inputs may be any that keep to these rules, and one draw needn't show every extreme that they name: `dest`: in the rows of one device (aligned blocks of 64 rows, in order), each owner is named by at most 24 rows, a bound that some block reaches. Let a = k // (256 / (2 * 4)) for a kept id k, and let x-slab p hold x from p * 256 / 4 on, 256 / 4 of them. When a >= 4, the cells on which row a of H(256) is nonzero lie in one x-slab. Among the 64 ids of one y-slab and one index of sta, at most 32 ids with a >= 4 touch any one x-slab, and some x-slab is touched by exactly 32.
All inputs are finite; a program needn't handle non-finite values.
Results may differ from a plain program's by a relative error of at most 0.0003.
Values sent between devices are 32-bit elements; how exact they have to be, the bound alone decides.
A program may use at most 128 MiB of HBM per device.

v0:
```python
import functools

import jax
import jax.numpy as jnp
from jax import lax
from jax.experimental import pallas as pl
from jax.experimental.pallas import tpu as pltpu
from jax.sharding import PartitionSpec as P

kernel_scale = 32.0
MESH = pl.DeviceIdType.MESH


def log2(n):
    return n.bit_length() - 1


def pyramid(pairs, level):
    return 2 * pairs - (2 * pairs >> level)


def row_plan(ids, j, me, slab, half, x_cells, y_cells):
    ls = log2(slab)
    pairs = x_cells // slab // 2
    a = ids >> log2(half)
    pair = j * half + (ids & (half - 1))
    total = pyramid(pairs, log2(pairs))
    first = jnp.full(a.shape, total, jnp.int32)
    second = jnp.full(a.shape, total, jnp.int32)
    factor = jnp.full(a.shape, x_cells ** -0.5, jnp.float32)
    turn = jnp.full(a.shape, 1.0, jnp.float32)
    back = jnp.full(a.shape, 0.0, jnp.float32)
    m = 1
    while m < x_cells:
        e = log2(m)
        at = a >= m
        k = a - m
        norm = (m / x_cells) ** 0.5
        if m >= slab:
            sh = e - ls
            mine = (k >> sh) == me
            here = k & ((1 << sh) - 1)
            factor = jnp.where(at, jnp.where(mine, norm, 0.0), factor)
            width = x_cells // m
            if width == 2:
                first = jnp.where(at, here, first)
                second = jnp.where(at, here, second)
                turn = jnp.where(at, -1.0, turn)
                back = jnp.where(at, 0.0, back)
            else:
                off = pyramid(pairs, log2(width) - 2)
                first = jnp.where(at, off + 2 * here, first)
                second = jnp.where(at, off + 2 * here + 1, second)
                back = jnp.where(at, -1.0, back)
        else:
            sh = ls - e
            mine = k == (me >> sh)
            sign = norm * (1 - 2 * ((me >> (sh - 1)) & 1)).astype(jnp.float32)
            factor = jnp.where(at, jnp.where(mine, sign, 0.0), factor)
        m = m * 2
    ynorm = jnp.full(a.shape, y_cells ** -0.5, jnp.float32)
    m = 1
    while m < y_cells // 2:
        ynorm = jnp.where(pair >= m, (2 * m / y_cells) ** 0.5, ynorm)
        m = m * 2

    def address(row):
        at = ((row & ~7) + pair) * y_cells + (row & 7)
        m = 16
        while m < y_cells:
            k = 2 * pair - m
            wide = m // 8
            spot = 8 * (wide + (k & (wide - 1))) + (k >> log2(wide))
            at = jnp.where(k >= 0, row * y_cells + spot, at)
            m = m * 2
        return at

    factor = factor * ynorm
    return address(first), address(second), factor, factor * turn, back


def z_matrix(z_cells, t):
    z = lax.broadcasted_iota(jnp.int32, (2 * z_cells, 2 * z_cells), 0) & (z_cells - 1)
    lane = lax.broadcasted_iota(jnp.int32, (2 * z_cells, 2 * z_cells), 1)
    c = lane & (z_cells - 1)
    value = jnp.full(z.shape, z_cells ** -0.5, jnp.float32)
    m = 1
    while m < z_cells:
        w = log2(z_cells // m)
        k = c - m
        norm = (m / z_cells) ** 0.5
        hit = (z >> w) == k
        up = ((z >> (w - 1)) & 1) == 0
        value = jnp.where(c >= m, jnp.where(hit, jnp.where(up, norm, -norm), 0.0), value)
        m = m * 2
    return jnp.where((lane >> log2(z_cells)) == t, value, 0.0)


def tree(values):
    out = [None] * len(values)
    while len(values) > 1:
        half = len(values) // 2
        for k in range(half):
            out[half + k] = values[2 * k] - values[2 * k + 1]
        values = [values[2 * k] + values[2 * k + 1] for k in range(half)]
    out[0] = values[0]
    return out


GROUP = 4
CHUNK = 8


def whole_kernel(
    sizes, place, height, w_hbm, kept, dest, out,
    field, sums, halves, weights, turned, table, select, others, rows_v, rows_s, scale_v, back_v,
    taken, given, parts, arrived, packed,
    w_sem, row_sem, i_send, i_recv, s_send, s_recv, o_send, o_recv, own_sem,
):
    slab, owners, stations, keep, x_local, y_cells, z_cells, capacity = sizes
    lanes = 2 * z_cells
    pairs = x_local // 2
    rows_x = 2 * pairs
    groups = pairs // GROUP
    chunks = x_local // CHUNK
    x_cells = x_local * slab
    half = y_cells // slab // 2
    per_row = stations * keep
    runs = y_cells // 8
    me, q = lax.axis_index("slab"), lax.axis_index("sta")
    plane = rows_x * y_cells
    left = lax.broadcasted_iota(jnp.int32, (8, lanes), 1) < z_cells
    zed = (lax.broadcasted_iota(jnp.int32, (8, lanes), 1) & (z_cells - 1)).astype(jnp.float32) + 0.5
    beside = jnp.where(left, 0.5, 1.5)

    def before(d):
        return lax.rem(me - d + slab, slab)

    def id_copy(d):
        return pltpu.make_async_remote_copy(
            src_ref=kept.at[0],
            dst_ref=others.at[d - 1],
            send_sem=i_send.at[d - 1],
            recv_sem=i_recv.at[d - 1],
            device_id=(lax.rem(me + d, slab), q),
            device_id_type=MESH,
        )

    def part_copy(d):
        return pltpu.make_async_remote_copy(
            src_ref=parts.at[d],
            dst_ref=arrived.at[d - 1],
            send_sem=s_send.at[d - 1],
            recv_sem=s_recv.at[d - 1],
            device_id=(before(d), q),
            device_id_type=MESH,
        )

    def out_copy(d):
        to = lax.rem(q + d, owners)
        return pltpu.make_async_remote_copy(
            src_ref=packed.at[to],
            dst_ref=out.at[q],
            send_sem=o_send.at[d - 1],
            recv_sem=o_recv.at[d - 1],
            device_id=(me, to),
            device_id_type=MESH,
        )

    def row_copy():
        return pltpu.make_async_copy(rows_v, rows_s, row_sem)

    def w_copy(c):
        return pltpu.make_async_copy(
            w_hbm.at[pl.ds(c * CHUNK, CHUNK)], weights.at[pl.ds(c * CHUNK, CHUNK)], w_sem.at[c]
        )

    for c in range(chunks):
        w_copy(c).start()
    barrier = pltpu.get_barrier_semaphore()
    for d in range(1, slab):
        pl.semaphore_signal(
            barrier, inc=1, device_id=(lax.rem(me + d, slab), q), device_id_type=MESH
        )
    for d in range(1, owners):
        pl.semaphore_signal(
            barrier, inc=1, device_id=(me, lax.rem(q + d, owners)), device_id_type=MESH
        )

    base = (lax.broadcasted_iota(jnp.int32, (8, lanes), 0) * runs).astype(jnp.float32) + 0.5
    for s in range(stations):
        depth = zed + height[s]
        square = depth * depth
        north = base - place[1, s] * y_cells
        for r in range(runs):
            n = north + float(r)
            table[s, r] = n * n + square
    owner = jnp.zeros((1, per_row), jnp.float32)
    for s in range(stations):
        spread = lax.broadcasted_iota(jnp.int32, (keep, per_row), 1) == (
            lax.broadcasted_iota(jnp.int32, (keep, per_row), 0) + s * keep
        )
        owner = owner + jnp.dot(
            dest[s].astype(jnp.float32), spread.astype(jnp.float32),
            preferred_element_type=jnp.float32,
        )
    names = lax.broadcasted_iota(jnp.int32, (owners, per_row), 0).astype(jnp.float32)
    named = (names == owner).astype(jnp.float32)
    earlier = (
        lax.broadcasted_iota(jnp.int32, (per_row, per_row), 0)
        < lax.broadcasted_iota(jnp.int32, (per_row, per_row), 1)
    ).astype(jnp.float32)
    rank = jnp.dot(named, earlier, preferred_element_type=jnp.float32)
    slot = jnp.sum(rank * named, axis=0, keepdims=True)
    spot = owner * capacity + slot
    rows = lax.broadcasted_iota(jnp.int32, (owners * capacity, per_row), 0).astype(jnp.float32)
    select[...] = (rows == spot).astype(jnp.float32)

    def turn_chunk(c, carry):
        w_copy(c).wait()
        for u in range(CHUNK // 2):
            for h in range(y_cells // 128):
                tall = jnp.concatenate(
                    [weights[c * CHUNK + 2 * u + i, :, h * 128 : (h + 1) * 128] for i in range(2)], axis=0
                ).T
                at = (c * (CHUNK // 2) + u) * y_cells
                for k in range(128 // runs):
                    turned[pl.ds(at + h * (128 // runs) + k, runs, stride=8), :] = tall[
                        k * runs : (k + 1) * runs
                    ]
        return carry

    lax.fori_loop(0, chunks, turn_chunk, 0)

    def ready():
        pl.semaphore_wait(barrier, slab + owners - 2)
        for d in range(1, slab):
            id_copy(d).start()

    def plan():
        for d in range(1, slab):
            id_copy(d).wait()
        lane = lax.broadcasted_iota(jnp.int32, (stations, per_row), 1) >> log2(keep)
        line = lane == lax.broadcasted_iota(jnp.int32, (stations, per_row), 0)
        flat = []
        for d in range(slab):
            ids = kept[0] if d == 0 else others[d - 1]
            wide = jnp.where(line, jnp.concatenate([ids] * stations, axis=1), 0)
            one = wide[0:1]
            for s in range(1, stations):
                one = one + wide[s : s + 1]
            flat.append(one)
        flat = jnp.concatenate(flat, axis=0)
        j = lax.broadcasted_iota(jnp.int32, (slab, per_row), 0)
        j = lax.rem(me - j + slab, slab)
        first, second, f0, f1, back = row_plan(flat, j, me, slab, half, x_cells, y_cells)
        rows_v[0] = first
        rows_v[1] = second
        row_copy().start()
        tall = jnp.concatenate([f0, f1, back, back], axis=0)
        tall = jnp.concatenate([tall, jnp.zeros((4 * slab, 128 - per_row), jnp.float32)], axis=1).T
        side = lax.broadcasted_iota(jnp.int32, (per_row, lanes), 1) < z_cells
        for d in range(slab):
            f0 = tall[:per_row, d : d + 1]
            f1 = tall[:per_row, slab + d : slab + d + 1]
            scale = jnp.where(side, f0, f1)
            for s in range(stations):
                z_part = kernel_scale * (zed[0:1] + height[s])
                scale_v[d, s * keep : (s + 1) * keep] = scale[s * keep : (s + 1) * keep] * z_part
            back_v[d] = jnp.broadcast_to(tall[:per_row, 2 * slab + d : 2 * slab + d + 1], (per_row, lanes))

    def station(s, carry):
        pl.when(s == 1)(ready)
        pl.when(s == stations - 1)(plan)
        east = (me * x_local).astype(jnp.float32) - place[0, s] * x_cells

        def where(row, v):
            if v == 0:
                return sums, (s * rows_x + row) * 8
            if v == 1:
                return halves, (s * rows_x + row) * 8
            return field, s * plane + row * y_cells + v * 8

        def put(row, v, value):
            ref, at = where(row, v)
            ref[pl.ds(pl.multiple_of(at, 8), 8), :] = value

        def get(row, v):
            ref, at = where(row, v)
            return ref[pl.ds(pl.multiple_of(at, 8), 8), :]

        for g in range(groups):
            easts = []
            for u in range(GROUP):
                e = beside + (east + float(2 * (g * GROUP + u)))
                easts.append(e * e)

            def emit(v, values):
                level, at = 0, g * GROUP
                while True:
                    for i, value in enumerate(values):
                        put(pyramid(pairs, level) + at + i, v, value)
                    if len(values) == 1:
                        break
                    values = [values[2 * i] + values[2 * i + 1] for i in range(len(values) // 2)]
                    level, at = level + 1, at // 2
                value = values[0]
                while at & 1:
                    value = get(pyramid(pairs, level) + at - 1, v) + value
                    level, at = level + 1, at // 2
                    put(pyramid(pairs, level) + at, v, value)

            stack = []
            for r in range(runs):
                t = table[s, r]
                values = []
                for u in range(GROUP):
                    inv = lax.rsqrt(t + easts[u])
                    w = turned[pl.ds(((g * GROUP + u) * runs + r) * 8, 8), :]
                    values.append((w * inv) * (inv * inv))
                level, run = 0, r
                while stack and stack[-1][0] == level:
                    _, other = stack.pop()
                    level, run = level + 1, run >> 1
                    emit((runs >> level) + run, [o - v for o, v in zip(other, values)])
                    values = [o + v for o, v in zip(other, values)]
                stack.append((level, values))
            emit(0, stack[0][1])
        return carry

    lax.fori_loop(0, stations, station, 0)

    def finish_y(tile, carry):
        at = pl.multiple_of(tile * 64, 64)
        values = tree([sums[pl.ds(at + i, 8, stride=8), :] for i in range(8)])
        values = values + [halves[pl.ds(at + i, 8, stride=8), :] for i in range(8)]
        for b in range(16):
            to = (tile * 8 + b // 2) * y_cells + (b % 2) * 8
            field[pl.ds(pl.multiple_of(to, 8), 8), :] = values[b]
        return carry

    lax.fori_loop(0, stations * rows_x // 8, finish_y, 0)

    turn_z = jnp.concatenate([z_matrix(z_cells, 0), z_matrix(z_cells, 1)], axis=0)
    row_copy().wait()

    def part(d):
        for s in range(stations):
            for i in range(keep):
                k = s * keep + i
                taken[2 * k : 2 * k + 2, :] = field[pl.ds(s * plane + rows_s[0, d, k], 2, stride=8), :]
                given[2 * k : 2 * k + 2, :] = field[pl.ds(s * plane + rows_s[1, d, k], 2, stride=8), :]
        back, scale = back_v[d], scale_v[d]
        sides = [
            (taken[pl.ds(t, per_row, stride=2), :] + back * given[pl.ds(t, per_row, stride=2), :]) * scale
            for t in range(2)
        ]
        return jnp.dot(
            jnp.concatenate(sides, axis=1), turn_z,
            precision=lax.Precision.HIGHEST, preferred_element_type=jnp.float32,
        )

    def send_part(d, carry):
        parts[d] = part(d)
        part_copy(d).start()
        return carry

    lax.fori_loop(1, slab, send_part, 0)
    total = part(0)
    for d in range(1, slab):
        part_copy(d).wait()
        total = total + arrived[d - 1]
    packed[...] = jnp.dot(
        select[...], total, precision=lax.Precision.HIGHEST, preferred_element_type=jnp.float32
    ).reshape(packed.shape)
    for d in range(1, owners):
        out_copy(d).start()
    own = pltpu.make_async_copy(packed.at[q], out.at[q], own_sem)
    own.start()
    own.wait()
    for d in range(1, owners):
        out_copy(d).wait()


def local(station_place, station_height, cell_weight, kept, dest):
    slab = lax.axis_size("slab")
    owners = lax.axis_size("sta")
    x_local, y_cells, z_cells = cell_weight.shape
    stations = station_place.shape[0]
    keep = kept.shape[2]
    lanes = 2 * z_cells
    per_row = stations * keep
    capacity = max(2, 3 * per_row // owners)
    sizes = (slab, owners, stations, keep, x_local, y_cells, z_cells, capacity)
    dma = pltpu.SemaphoreType.DMA
    out = pl.pallas_call(
        functools.partial(whole_kernel, sizes),
        out_shape=jax.ShapeDtypeStruct((owners, capacity, lanes), jnp.float32),
        in_specs=[
            pl.BlockSpec(memory_space=pltpu.SMEM),
            pl.BlockSpec(memory_space=pltpu.SMEM),
            pl.BlockSpec(memory_space=pl.ANY),
            pl.BlockSpec(memory_space=pltpu.VMEM),
            pl.BlockSpec(memory_space=pltpu.VMEM),
        ],
        out_specs=pl.BlockSpec(memory_space=pl.ANY),
        scratch_shapes=[
            pltpu.VMEM((stations * x_local * y_cells, lanes), jnp.float32),
            pltpu.VMEM((stations * x_local * 8, lanes), jnp.float32),
            pltpu.VMEM((stations * x_local * 8, lanes), jnp.float32),
            pltpu.VMEM((x_local, z_cells, y_cells), jnp.float32),
            pltpu.VMEM((x_local // 2 * y_cells, lanes), jnp.float32),
            pltpu.VMEM((stations, y_cells // 8, 8, lanes), jnp.float32),
            pltpu.VMEM((owners * capacity, per_row), jnp.float32),
            pltpu.VMEM((slab - 1, stations, keep), jnp.int32),
            pltpu.VMEM((2, slab, per_row), jnp.int32),
            pltpu.SMEM((2, slab, per_row), jnp.int32),
            pltpu.VMEM((slab, per_row, lanes), jnp.float32),
            pltpu.VMEM((slab, per_row, lanes), jnp.float32),
            pltpu.VMEM((2 * per_row, lanes), jnp.float32),
            pltpu.VMEM((2 * per_row, lanes), jnp.float32),
            pltpu.VMEM((slab, per_row, lanes), jnp.float32),
            pltpu.VMEM((slab - 1, per_row, lanes), jnp.float32),
            pltpu.VMEM((owners, capacity, lanes), jnp.float32),
            dma((x_local // CHUNK,)),
            dma,
            dma((slab - 1,)),
            dma((slab - 1,)),
            dma((slab - 1,)),
            dma((slab - 1,)),
            dma((owners - 1,)),
            dma((owners - 1,)),
            dma,
        ],
        compiler_params=pltpu.CompilerParams(
            collective_id=0, has_side_effects=True, vmem_limit_bytes=60 * 1024 * 1024
        ),
    )(
        jnp.transpose(station_place),
        station_height,
        jnp.transpose(cell_weight, (0, 2, 1)),
        kept,
        jnp.transpose(dest, (0, 1, 3, 2)).reshape(stations, 1, keep),
    )
    return out.reshape(1, 1, owners, capacity, lanes)


def solution(mesh):
    placed = (
        P("sta", None),
        P("sta"),
        P("slab", None, None),
        P("slab", "sta", None),
        P("slab", "sta", None, None),
    )
    return jax.shard_map(
        local,
        mesh=mesh,
        in_specs=placed,
        out_specs=P("slab", "sta", None, None, None),
        check_vma=False,
    )
```

profile of v0, /device:TPU:0, one launch (start us, length us, event | category | flops | bytes accessed | tf_op | source)
XLA Modules:
  0.0 23.6 jit_solution(5104787992188818873)
XLA Ops:
  0.0 22.0 %shard_map.55 = f32[8,24,128]{2,1,0:T(8,128)} custom-call(f32[2,4]{1,0:T(2,128)} %bitcast.9, f32[4]{0:T(128)} %height.1, f32[64,64,256]{2,1,0:T(8,128)} %bitcast.6, s32[1,4,16]{2,1,0:T(4,128)} %kept.1, s32[4,1,16]{2,1,0:T(1,128)} %bitcast.8), custom_call_target="tpu_custom_call" | custom-call | tf_op jit(solution)/shard_map/pallas_call | solution.py:396
  22.0 1.5 %copy.8 = f32[1,1,8,24,128]{4,3,2,1,0:T(8,128)} copy(f32[1,1,8,24,128]{4,3,2,1,0:T(8,128)} %bitcast.7) | data formatting | bytes 196608
where the time goes:
time: 23.7 us; the launch traced here: 23.6 us
  Pallas kernels  22 us (93%)
  local copies, waits for them, and re-layouts  1.54 us (6%)
    pallas_call x1, Pallas kernels, local(): pl.pallas_call(functools.partial(whole_kernel, sizes), out_shape=jax.Shap...  22 us
    unnamed x1, local copies, waits for them, and re-layouts  1.54 us

commit v1 on v0

--- a/solution.py
+++ b/solution.py
@@ -395,7 +395,7 @@
     dma = pltpu.SemaphoreType.DMA
     out = pl.pallas_call(
         functools.partial(whole_kernel, sizes),
-        out_shape=jax.ShapeDtypeStruct((owners, capacity, lanes), jnp.float32),
+        out_shape=pltpu.VMEM((owners, capacity, lanes), jnp.float32),
         in_specs=[
             pl.BlockSpec(memory_space=pltpu.SMEM),
             pl.BlockSpec(memory_space=pltpu.SMEM),
@@ -433,14 +433,19 @@
             dma,
         ],
         compiler_params=pltpu.CompilerParams(
-            collective_id=0, has_side_effects=True, vmem_limit_bytes=60 * 1024 * 1024
+            collective_id=0, has_side_effects=True, vmem_limit_bytes=48_000_000
         ),
     )(
-        jnp.transpose(station_place),
-        station_height,
-        jnp.transpose(cell_weight, (0, 2, 1)),
-        kept,
-        jnp.transpose(dest, (0, 1, 3, 2)).reshape(stations, 1, keep),
+        *(
+            pltpu.with_memory_space_constraint(a, pltpu.HBM)
+            for a in (
+                jnp.transpose(station_place),
+                station_height,
+                jnp.transpose(cell_weight, (0, 2, 1)),
+                kept,
+                jnp.transpose(dest, (0, 1, 3, 2)).reshape(stations, 1, keep),
+            )
+        )
     )
     return out.reshape(1, 1, owners, capacity, lanes)
 

time: 23.7 us -> 22.7 us (0.958)
  local copies, waits for them, and re-layouts: 1.54 us -> 0.64 us
    unnamed x1, local copies, waits for them, and re-layouts: 1.54 us -> 0.64 us
where the time goes in v1:
time: 22.7 us; the launch traced here: 22.6 us
  Pallas kernels  21.9 us (96%)
  local copies, waits for them, and re-layouts  0.64 us (3%)
    pallas_call x1, Pallas kernels, local(): pl.pallas_call(functools.partial(whole_kernel, sizes), out_shape=pltpu.VM...  21.9 us
    unnamed x1, local copies, waits for them, and re-layouts  0.64 us

profile of v1, /device:TPU:0, one launch (start us, length us, event | category | flops | bytes accessed | tf_op | source)
XLA Modules:
  0.0 22.6 jit_solution(16786167875244531035)
XLA Ops:
  0.0 21.9 %shard_map.55 = f32[8,24,128]{2,1,0:T(8,128)S(1)} custom-call(f32[2,4]{1,0:T(2,128)} %bitcast.9, f32[4]{0:T(128)} %height.1, f32[64,64,256]{2,1,0:T(8,128)} %bitcast.7, s32[1,4,16]{2,1,0:T(4,128)} %kept.1, s32[4,1,16]{2,1,0:T(1,128)} %bitcast.8), custom_call_target="tpu_custom_call" | custom-call | tf_op jit(solution)/shard_map/pallas_call | solution.py:396
  21.9 0.6 %copy.8 = f32[1,1,8,24,128]{4,3,2,1,0:T(8,128)} copy(f32[1,1,8,24,128]{4,3,2,1,0:T(8,128)S(1)} %bitcast.6) | data formatting | bytes 196608

commit v2 on v1

v2 whole, which is shorter than its diff:
```python
import functools

import jax
import jax.numpy as jnp
from jax import lax
from jax.experimental import pallas as pl
from jax.experimental.pallas import tpu as pltpu
from jax.sharding import PartitionSpec as P

kernel_scale = 32.0
MESH = pl.DeviceIdType.MESH


def log2(n):
    return n.bit_length() - 1


def pyramid(pairs, level):
    return 2 * pairs - (2 * pairs >> level)


def row_plan(ids, j, me, slab, half, x_cells, y_cells):
    ls = log2(slab)
    pairs = x_cells // slab // 2
    a = ids >> log2(half)
    pair = j * half + (ids & (half - 1))
    total = pyramid(pairs, log2(pairs))
    first = jnp.full(a.shape, total, jnp.int32)
    second = jnp.full(a.shape, total, jnp.int32)
    factor = jnp.full(a.shape, x_cells ** -0.5, jnp.float32)
    turn = jnp.full(a.shape, 1.0, jnp.float32)
    back = jnp.full(a.shape, 0.0, jnp.float32)
    m = 1
    while m < x_cells:
        e = log2(m)
        at = a >= m
        k = a - m
        norm = (m / x_cells) ** 0.5
        if m >= slab:
            sh = e - ls
            mine = (k >> sh) == me
            here = k & ((1 << sh) - 1)
            factor = jnp.where(at, jnp.where(mine, norm, 0.0), factor)
            width = x_cells // m
            if width == 2:
                first = jnp.where(at, here, first)
                second = jnp.where(at, here, second)
                turn = jnp.where(at, -1.0, turn)
                back = jnp.where(at, 0.0, back)
            else:
                off = pyramid(pairs, log2(width) - 2)
                first = jnp.where(at, off + 2 * here, first)
                second = jnp.where(at, off + 2 * here + 1, second)
                back = jnp.where(at, -1.0, back)
        else:
            sh = ls - e
            mine = k == (me >> sh)
            sign = norm * (1 - 2 * ((me >> (sh - 1)) & 1)).astype(jnp.float32)
            factor = jnp.where(at, jnp.where(mine, sign, 0.0), factor)
        m = m * 2
    ynorm = jnp.full(a.shape, y_cells ** -0.5, jnp.float32)
    m = 1
    while m < y_cells // 2:
        ynorm = jnp.where(pair >= m, (2 * m / y_cells) ** 0.5, ynorm)
        m = m * 2

    def address(row):
        at = ((row & ~7) + pair) * y_cells + (row & 7)
        m = 16
        while m < y_cells:
            k = 2 * pair - m
            wide = m // 8
            spot = 8 * (wide + (k & (wide - 1))) + (k >> log2(wide))
            at = jnp.where(k >= 0, row * y_cells + spot, at)
            m = m * 2
        return at

    factor = factor * ynorm
    return address(first), address(second), factor, factor * turn, back


def z_signs(z_cells, t):
    z = lax.broadcasted_iota(jnp.int32, (2 * z_cells, 2 * z_cells), 0) & (z_cells - 1)
    lane = lax.broadcasted_iota(jnp.int32, (2 * z_cells, 2 * z_cells), 1)
    c = lane & (z_cells - 1)
    value = jnp.full(z.shape, 1.0, jnp.float32)
    m = 1
    while m < z_cells:
        w = log2(z_cells // m)
        k = c - m
        hit = (z >> w) == k
        up = ((z >> (w - 1)) & 1) == 0
        value = jnp.where(c >= m, jnp.where(hit, jnp.where(up, 1.0, -1.0), 0.0), value)
        m = m * 2
    return jnp.where((lane >> log2(z_cells)) == t, value, 0.0)


def z_norms(z_cells):
    c = lax.broadcasted_iota(jnp.int32, (8, 2 * z_cells), 1) & (z_cells - 1)
    norm = jnp.full(c.shape, z_cells ** -0.5, jnp.float32)
    m = 1
    while m < z_cells:
        norm = jnp.where(c >= m, (m / z_cells) ** 0.5, norm)
        m = m * 2
    return norm


def pieces(x):
    high = x.astype(jnp.bfloat16)
    rest = x - high.astype(jnp.float32)
    middle = rest.astype(jnp.bfloat16)
    low = (rest - middle.astype(jnp.float32)).astype(jnp.bfloat16)
    return jnp.concatenate([high, middle, low], axis=0)


def tree(values):
    out = [None] * len(values)
    while len(values) > 1:
        half = len(values) // 2
        for k in range(half):
            out[half + k] = values[2 * k] - values[2 * k + 1]
        values = [values[2 * k] + values[2 * k + 1] for k in range(half)]
    out[0] = values[0]
    return out


GROUP = 4
CHUNK = 2 * GROUP


def whole_kernel(
    sizes, place_h, height_h, w_hbm, kept_h, dest_h, out,
    fields, sums, halves, place, height, kept, dest,
    weights, turned, table, select, signs, others, rows_v, rows_s, scale_v, back_v,
    taken, given, parts, arrived, packed,
    w_sem, in_sem, row_sem, i_send, i_recv, s_send, s_recv, o_send, o_recv, own_sem,
):
    slab, owners, stations, keep, x_local, y_cells, z_cells, capacity = sizes
    lanes = 2 * z_cells
    pairs = x_local // 2
    rows_x = 2 * pairs
    groups = pairs // GROUP
    x_cells = x_local * slab
    half = y_cells // slab // 2
    per_row = stations * keep
    runs = y_cells // 8
    me, q = lax.axis_index("slab"), lax.axis_index("sta")
    zed = (lax.broadcasted_iota(jnp.int32, (8, lanes), 1) & (z_cells - 1)).astype(jnp.float32) + 0.5

    def before(d):
        return lax.rem(me - d + slab, slab)

    def id_copy(d):
        return pltpu.make_async_remote_copy(
            src_ref=kept,
            dst_ref=others.at[d - 1],
            send_sem=i_send.at[d - 1],
            recv_sem=i_recv.at[d - 1],
            device_id=(lax.rem(me + d, slab), q),
            device_id_type=MESH,
        )

    def part_copy(s, d):
        return pltpu.make_async_remote_copy(
            src_ref=parts.at[s, d],
            dst_ref=arrived.at[s, d - 1],
            send_sem=s_send.at[s, d - 1],
            recv_sem=s_recv.at[s, d - 1],
            device_id=(before(d), q),
            device_id_type=MESH,
        )

    def out_copy(d):
        to = lax.rem(q + d, owners)
        return pltpu.make_async_remote_copy(
            src_ref=packed.at[to],
            dst_ref=out.at[q],
            send_sem=o_send.at[d - 1],
            recv_sem=o_recv.at[d - 1],
            device_id=(me, to),
            device_id_type=MESH,
        )

    def row_copy():
        return pltpu.make_async_copy(rows_v, rows_s, row_sem)

    def w_copy(c):
        return pltpu.make_async_copy(
            w_hbm.at[pl.ds(c * CHUNK, CHUNK)], weights.at[pl.ds(c * CHUNK, CHUNK)], w_sem.at[c]
        )

    inputs = [
        pltpu.make_async_copy(a, b, in_sem.at[i])
        for i, (a, b) in enumerate(
            [(place_h, place), (height_h, height), (kept_h.at[0], kept), (dest_h, dest)]
        )
    ]
    for copy in inputs:
        copy.start()
    for c in range(groups):
        w_copy(c).start()
    barrier = pltpu.get_barrier_semaphore()
    for d in range(1, slab):
        pl.semaphore_signal(
            barrier, inc=1, device_id=(lax.rem(me + d, slab), q), device_id_type=MESH
        )
    for d in range(1, owners):
        pl.semaphore_signal(
            barrier, inc=1, device_id=(me, lax.rem(q + d, owners)), device_id_type=MESH
        )
    signs[...] = jnp.concatenate([z_signs(z_cells, 0), z_signs(z_cells, 1)], axis=0).astype(jnp.bfloat16)
    for copy in inputs:
        copy.wait()

    def heights(s):
        base = (lax.broadcasted_iota(jnp.int32, (8, lanes), 0) * runs).astype(jnp.float32) + 0.5
        depth = zed + height[s]
        square = depth * depth
        north = base - place[1, s] * y_cells
        for r in range(runs):
            n = north + float(r)
            table[s, r] = n * n + square

    def choose():
        owner = jnp.zeros((1, per_row), jnp.float32)
        for s in range(stations):
            spread = lax.broadcasted_iota(jnp.int32, (keep, per_row), 1) == (
                lax.broadcasted_iota(jnp.int32, (keep, per_row), 0) + s * keep
            )
            owner = owner + jnp.dot(
                dest[s].astype(jnp.float32), spread.astype(jnp.float32),
                preferred_element_type=jnp.float32,
            )
        names = lax.broadcasted_iota(jnp.int32, (owners, per_row), 0).astype(jnp.float32)
        named = (names == owner).astype(jnp.float32)
        earlier = (
            lax.broadcasted_iota(jnp.int32, (per_row, per_row), 0)
            < lax.broadcasted_iota(jnp.int32, (per_row, per_row), 1)
        ).astype(jnp.float32)
        rank = jnp.dot(named, earlier, preferred_element_type=jnp.float32)
        slot = jnp.sum(rank * named, axis=0, keepdims=True)
        spot = owner * capacity + slot
        rows = lax.broadcasted_iota(jnp.int32, (owners * capacity, per_row), 0).astype(jnp.float32)
        chosen = (rows == spot).astype(jnp.float32)
        cut = (stations - 1) * keep
        wide = jnp.concatenate([chosen[:, :cut]] * 3 + [chosen[:, cut:]] * 3, axis=1)
        select[...] = wide.astype(jnp.bfloat16)

    def push(c, u, h):
        return jnp.concatenate(
            [weights[c * CHUNK + 2 * u + i, :, h * 128 : (h + 1) * 128] for i in range(2)], axis=0
        ).T

    def drop(c, u, h, tall):
        for k in range(128 // runs):
            turned[c * GROUP + u, pl.ds(h * (128 // runs) + k, runs, stride=8), :] = tall[
                k * runs : (k + 1) * runs
            ]

    tiles = [(u, h) for u in range(GROUP) for h in range(y_cells // 128)]

    def ready():
        pl.semaphore_wait(barrier, slab + owners - 2)
        for d in range(1, slab):
            id_copy(d).start()

    held = {}

    def plan_ids():
        for d in range(1, slab):
            id_copy(d).wait()

    def plan_rows():
        lane = lax.broadcasted_iota(jnp.int32, (stations, per_row), 1) >> log2(keep)
        line = lane == lax.broadcasted_iota(jnp.int32, (stations, per_row), 0)
        flat = []
        for d in range(slab):
            ids = kept[...] if d == 0 else others[d - 1]
            wide = jnp.where(line, jnp.concatenate([ids] * stations, axis=1), 0)
            one = wide[0:1]
            for s in range(1, stations):
                one = one + wide[s : s + 1]
            flat.append(one)
        flat = jnp.concatenate(flat, axis=0)
        j = lax.broadcasted_iota(jnp.int32, (slab, per_row), 0)
        j = lax.rem(me - j + slab, slab)
        first, second, f0, f1, back = row_plan(flat, j, me, slab, half, x_cells, y_cells)
        rows_v[0] = first
        rows_v[1] = second
        tall = jnp.concatenate([f0, f1, back, back], axis=0)
        tall = jnp.concatenate([tall, jnp.zeros((4 * slab, 128 - per_row), jnp.float32)], axis=1)
        held["tall"] = tall.T

    def plan_scale(s, d):
        tall = held["tall"]
        side = lax.broadcasted_iota(jnp.int32, (keep, lanes), 1) < z_cells
        z_part = kernel_scale * (zed[0:1] + height[s])
        k = s * keep
        f0 = tall[k : k + keep, d : d + 1]
        f1 = tall[k : k + keep, slab + d : slab + d + 1]
        back = tall[k : k + keep, 2 * slab + d : 2 * slab + d + 1]
        scale_v[s, d * keep : (d + 1) * keep] = jnp.where(side, f0, f1) * z_part
        back_v[s, d * keep : (d + 1) * keep] = jnp.broadcast_to(back, (keep, lanes))

    def finish_y(s, tile):
        at = (s * rows_x + tile * 8) * 8
        values = tree([sums[pl.ds(at + i, 8, stride=8), :] for i in range(8)])
        values = values + [halves[pl.ds(at + i, 8, stride=8), :] for i in range(8)]
        for b in range(16):
            to = (tile * 8 + b // 2) * y_cells + (b % 2) * 8
            fields[s][pl.ds(to, 8), :] = values[b]

    def last_group(row):
        level = 0
        while row >= pyramid(pairs, level + 1):
            level = level + 1
        return min(pairs - 1, ((row - pyramid(pairs, level) + 1) << level) - 1) // GROUP

    def finished(g):
        ready_at = [max(last_group(8 * t + i) for i in range(8)) for t in range(rows_x // 8)]
        return [t for t, at in enumerate(ready_at) if at == g]

    def gather(s, k):
        d, i = k // keep, k % keep
        for n in range(2):
            to = taken if n == 0 else given
            to[s, 2 * k : 2 * k + 2, :] = fields[s][pl.ds(rows_s[n, d, s * keep + i], 2, stride=8), :]

    blocks = slab * keep

    def depth_dot(s):
        back, scale = back_v[s], scale_v[s]
        sides = []
        for t in range(2):
            mine = pl.ds(t, blocks, stride=2)
            sides.append((taken[s, mine, :] + back * given[s, mine, :]) * scale)
        held[s] = jnp.dot(
            pieces(jnp.concatenate(sides, axis=1)), signs[...], preferred_element_type=jnp.float32
        )

    def send(s):
        tall = held.pop(s)
        rows = (tall[2 * blocks :] + tall[blocks : 2 * blocks]) + tall[:blocks]
        rows = rows * z_norms(z_cells)[0:1]
        for d in range(slab):
            parts[s, d] = rows[d * keep : (d + 1) * keep]
        for d in range(1, slab):
            part_copy(s, d).start()

    def total(s):
        value = parts[s, 0]
        for d in range(1, slab):
            part_copy(s, d).wait()
            value = value + arrived[s, d - 1]
        return value

    far = 2 * lax.broadcasted_iota(jnp.int32, (GROUP, 8, lanes), 0)
    far = far.astype(jnp.float32) + jnp.where(
        lax.broadcasted_iota(jnp.int32, (GROUP, 8, lanes), 2) < z_cells, 0.5, 1.5
    )

    def evaluate(s, g, before_run):
        east = (me * x_local).astype(jnp.float32) - place[0, s] * x_cells

        def where(row, v):
            if v == 0:
                return sums, (s * rows_x + row) * 8
            if v == 1:
                return halves, (s * rows_x + row) * 8
            return fields[s], row * y_cells + v * 8

        def put(row, v, value):
            ref, at = where(row, v)
            ref[pl.ds(at, 8), :] = value

        def get(row, v):
            ref, at = where(row, v)
            return ref[pl.ds(at, 8), :]

        e = far + (east + float(2 * g * GROUP))
        easts = e * e

        def emit(v, wide):
            values = [wide[i] for i in range(GROUP)]
            level, at = 0, g * GROUP
            while True:
                for i, value in enumerate(values):
                    put(pyramid(pairs, level) + at + i, v, value)
                if len(values) == 1:
                    break
                values = [values[2 * i] + values[2 * i + 1] for i in range(len(values) // 2)]
                level, at = level + 1, at // 2
            value = values[0]
            while at & 1:
                value = get(pyramid(pairs, level) + at - 1, v) + value
                level, at = level + 1, at // 2
                put(pyramid(pairs, level) + at, v, value)

        stack = []
        for r in range(runs):
            before_run(r)
            inv = lax.rsqrt(table[s, r] + easts)
            w = turned[g * GROUP : (g + 1) * GROUP, r * 8 : r * 8 + 8, :]
            values = (w * inv) * (inv * inv)
            level, run = 0, r
            while stack and stack[-1][0] == level:
                _, other = stack.pop()
                level, run = level + 1, run >> 1
                emit((runs >> level) + run, other - values)
                values = other + values
            stack.append((level, values))
        emit(0, stack[0][1])

    class Phase:
        def __init__(self, order):
            self.order, self.steps, self.work = order, len(order) * runs, {}

        def at(self, step, f, *args):
            step = min(int(step), self.steps - 1)
            self.work.setdefault(step, []).append(functools.partial(f, *args))

        def over(self, items, start, stop):
            for n, item in enumerate(items):
                self.at((start + (stop - start) * n / len(items)) * self.steps, *item)

        def tiles(self):
            for i, (s, g) in enumerate(self.order):
                if g < groups - 1:
                    for n, t in enumerate(finished(g)):
                        self.at((i + 1) * runs + 2 + 8 * n, finish_y, s, t)

        def run(self):
            for s in sorted({s for s, _ in self.order}):
                heights(s)
            for i, (s, g) in enumerate(self.order):
                def before_run(r, i=i):
                    for f in self.work.get(i * runs + r, ()):
                        f()
                evaluate(s, g, before_run)

    def tiles_after(s):
        return [(finish_y, s, t) for t in finished(groups - 1)]

    def gathers(s):
        return [(gather, s, k) for k in range(blocks)]

    def push_later(c, u, h):
        held[c, u, h] = push(c, u, h)

    def drop_later(c, u, h):
        drop(c, u, h, held.pop((c, u, h)))

    w_copy(0).wait()
    for u, h in tiles:
        drop(0, u, h, push(0, u, h))

    first = Phase([(s, g) for g in range(groups) for s in range(2)])
    for g in range(groups - 1):
        start = 2 * g * runs
        first.at(start, lambda c: w_copy(c).wait(), g + 1)
        for n, (u, h) in enumerate(tiles):
            first.at(start + 5 * n, push_later, g + 1, u, h)
            first.at(start + 5 * n + 18, drop_later, g + 1, u, h)
    first.at(2 * runs, ready)
    first.at(first.steps // 2, choose)
    first.tiles()
    first.run()

    second = Phase([(2, g) for g in range(groups)])
    second.over(tiles_after(0) + tiles_after(1), 0.0, 0.18)
    second.at(0.20 * second.steps, plan_ids)
    second.at(0.20 * second.steps, plan_rows)
    second.at(0.52 * second.steps, lambda: row_copy().start())
    second.over([(plan_scale, s, d) for s in range(stations) for d in range(slab)], 0.52, 0.70)
    second.at(0.70 * second.steps, lambda: row_copy().wait())
    second.over(gathers(0), 0.71, 0.99)
    second.tiles()
    second.run()

    third = Phase([(s, g) for s in range(3, stations) for g in range(groups)])
    third.over(tiles_after(2), 0.0, 0.1)
    third.at(0, depth_dot, 0)
    third.over(gathers(1), 0.02, 0.30)
    third.at(0.24 * third.steps, send, 0)
    third.at(0.31 * third.steps, depth_dot, 1)
    third.over(gathers(2), 0.33, 0.62)
    third.at(0.58 * third.steps, send, 1)
    third.at(0.64 * third.steps, depth_dot, 2)
    third.at(0.88 * third.steps, send, 2)
    third.tiles()
    third.run()

    for f, *args in tiles_after(3) + gathers(3):
        f(*args)
    depth_dot(3)
    send(3)
    most = jnp.concatenate([total(s) for s in range(stations - 1)], axis=0)
    cut = 3 * (stations - 1) * keep
    early = jnp.dot(select[:, :cut], pieces(most), preferred_element_type=jnp.float32)
    late = jnp.dot(
        select[:, cut:], pieces(total(stations - 1)), preferred_element_type=jnp.float32
    )
    packed[...] = (early + late).reshape(packed.shape)
    for d in range(1, owners):
        out_copy(d).start()
    own = pltpu.make_async_copy(packed.at[q], out.at[q], own_sem)
    own.start()
    own.wait()
    for d in range(1, owners):
        out_copy(d).wait()


def local(station_place, station_height, cell_weight, kept, dest):
    slab = lax.axis_size("slab")
    owners = lax.axis_size("sta")
    x_local, y_cells, z_cells = cell_weight.shape
    stations = station_place.shape[0]
    keep = kept.shape[2]
    lanes = 2 * z_cells
    per_row = stations * keep
    capacity = max(2, 3 * per_row // owners)
    sizes = (slab, owners, stations, keep, x_local, y_cells, z_cells, capacity)
    dma = pltpu.SemaphoreType.DMA
    f32, i32 = jnp.float32, jnp.int32
    out = pl.pallas_call(
        functools.partial(whole_kernel, sizes),
        out_shape=pltpu.VMEM((owners, capacity, lanes), f32),
        in_specs=[pl.BlockSpec(memory_space=pl.ANY)] * 5,
        out_specs=pl.BlockSpec(memory_space=pl.ANY),
        scratch_shapes=[
            [pltpu.VMEM((x_local * y_cells, lanes), f32)] * stations,
            pltpu.VMEM((stations * x_local * 8, lanes), f32),
            pltpu.VMEM((stations * x_local * 8, lanes), f32),
            pltpu.SMEM((2, stations), f32),
            pltpu.SMEM((stations,), f32),
            pltpu.VMEM((stations, keep), i32),
            pltpu.VMEM((stations, 1, keep), i32),
            pltpu.VMEM((x_local, z_cells, y_cells), f32),
            pltpu.VMEM((x_local // 2, y_cells, lanes), f32),
            pltpu.VMEM((stations, y_cells // 8, 8, lanes), f32),
            pltpu.VMEM((owners * capacity, 3 * per_row), jnp.bfloat16),
            pltpu.VMEM((2 * lanes, lanes), jnp.bfloat16),
            pltpu.VMEM((slab - 1, stations, keep), i32),
            pltpu.VMEM((2, slab, per_row), i32),
            pltpu.SMEM((2, slab, per_row), i32),
            pltpu.VMEM((stations, slab * keep, lanes), f32),
            pltpu.VMEM((stations, slab * keep, lanes), f32),
            pltpu.VMEM((stations, 2 * slab * keep, lanes), f32),
            pltpu.VMEM((stations, 2 * slab * keep, lanes), f32),
            pltpu.VMEM((stations, slab, keep, lanes), f32),
            pltpu.VMEM((stations, slab - 1, keep, lanes), f32),
            pltpu.VMEM((owners, capacity, lanes), f32),
            dma((x_local // CHUNK,)),
            dma((4,)),
            dma,
            dma((slab - 1,)),
            dma((slab - 1,)),
            dma((stations, slab - 1)),
            dma((stations, slab - 1)),
            dma((owners - 1,)),
            dma((owners - 1,)),
            dma,
        ],
        compiler_params=pltpu.CompilerParams(
            collective_id=0, has_side_effects=True, vmem_limit_bytes=52_000_000
        ),
    )(
        *(
            pltpu.with_memory_space_constraint(a, pltpu.HBM)
            for a in (
                jnp.transpose(station_place),
                station_height,
                jnp.transpose(cell_weight, (0, 2, 1)),
                kept,
                jnp.transpose(dest, (0, 1, 3, 2)).reshape(stations, 1, keep),
            )
        )
    )
    return out.reshape(1, 1, owners, capacity, lanes)


def solution(mesh):
    placed = (
        P("sta", None),
        P("sta"),
        P("slab", None, None),
        P("slab", "sta", None),
        P("slab", "sta", None, None),
    )
    return jax.shard_map(
        local,
        mesh=mesh,
        in_specs=placed,
        out_specs=P("slab", "sta", None, None, None),
        check_vma=False,
    )
```

time: 22.7 us -> 21.7 us (0.956)
  Pallas kernels: 21.9 us -> 20.9 us
    pallas_call x1, Pallas kernels: 21.9 us -> 20.9 us  [local(): pl.pallas_call(functools.partial(whole_kernel, sizes), out_shape=pltpu.VM...]
where the time goes in v2:
time: 21.7 us; the launch traced here: 21.6 us
  Pallas kernels  20.9 us (96%)
  local copies, waits for them, and re-layouts  0.64 us (3%)
    pallas_call x1, Pallas kernels, local(): pl.pallas_call(functools.partial(whole_kernel, sizes), out_shape=pltpu.VM...  20.9 us
    unnamed x1, local copies, waits for them, and re-layouts  0.64 us

profile of v2, /device:TPU:0, one launch (start us, length us, event | category | flops | bytes accessed | tf_op | source)
XLA Modules:
  0.0 21.6 jit_solution(15313769280213491630)
XLA Ops:
  0.0 20.9 %shard_map.55 = f32[8,24,128]{2,1,0:T(8,128)S(1)} custom-call(f32[2,4]{1,0:T(2,128)} %bitcast.9, f32[4]{0:T(128)} %height_h.1, f32[64,64,256]{2,1,0:T(8,128)} %bitcast.7, s32[1,4,16]{2,1,0:T(4,128)} %kept_h.1, s32[4,1,16]{2,1,0:T(1,128)} %bitcast.8), custom_call_target="tpu_custom_call" | custom-call | tf_op jit(solution)/shard_map/pallas_call | solution.py:525
  20.9 0.6 %copy.8 = f32[1,1,8,24,128]{4,3,2,1,0:T(8,128)} copy(f32[1,1,8,24,128]{4,3,2,1,0:T(8,128)S(1)} %bitcast.6) | data formatting | bytes 196608

commit v3 on v2

--- a/solution.py
+++ b/solution.py
@@ -287,7 +287,10 @@
         first, second, f0, f1, back = row_plan(flat, j, me, slab, half, x_cells, y_cells)
         rows_v[0] = first
         rows_v[1] = second
-        tall = jnp.concatenate([f0, f1, back, back], axis=0)
+        held["tall"] = [f0, f1, back, back]
+
+    def plan_turn():
+        tall = jnp.concatenate(held["tall"], axis=0)
         tall = jnp.concatenate([tall, jnp.zeros((4 * slab, 128 - per_row), jnp.float32)], axis=1)
         held["tall"] = tall.T
 
@@ -462,15 +465,15 @@
             first.at(start + 5 * n, push_later, g + 1, u, h)
             first.at(start + 5 * n + 18, drop_later, g + 1, u, h)
     first.at(2 * runs, ready)
-    first.at(first.steps // 2, choose)
     first.tiles()
     first.run()
 
     second = Phase([(2, g) for g in range(groups)])
     second.over(tiles_after(0) + tiles_after(1), 0.0, 0.18)
-    second.at(0.20 * second.steps, plan_ids)
-    second.at(0.20 * second.steps, plan_rows)
-    second.at(0.52 * second.steps, lambda: row_copy().start())
+    second.at(0.22 * second.steps, plan_ids)
+    second.at(0.22 * second.steps, plan_rows)
+    second.at(0.44 * second.steps, lambda: row_copy().start())
+    second.at(0.44 * second.steps, plan_turn)
     second.over([(plan_scale, s, d) for s in range(stations) for d in range(slab)], 0.52, 0.70)
     second.at(0.70 * second.steps, lambda: row_copy().wait())
     second.over(gathers(0), 0.71, 0.99)
@@ -481,10 +484,10 @@
     third.over(tiles_after(2), 0.0, 0.1)
     third.at(0, depth_dot, 0)
     third.over(gathers(1), 0.02, 0.30)
-    third.at(0.24 * third.steps, send, 0)
     third.at(0.31 * third.steps, depth_dot, 1)
     third.over(gathers(2), 0.33, 0.62)
-    third.at(0.58 * third.steps, send, 1)
+    third.at(0.50 * third.steps, send, 0)
+    third.at(0.50 * third.steps, send, 1)
     third.at(0.64 * third.steps, depth_dot, 2)
     third.at(0.88 * third.steps, send, 2)
     third.tiles()
@@ -494,6 +497,7 @@
         f(*args)
     depth_dot(3)
     send(3)
+    choose()
     most = jnp.concatenate([total(s) for s in range(stations - 1)], axis=0)
     cut = 3 * (stations - 1) * keep
     early = jnp.dot(select[:, :cut], pieces(most), preferred_element_type=jnp.float32)

time: 21.7 us -> 21.4 us (0.986)
  Pallas kernels: 20.9 us -> 20.6 us
    pallas_call x1, Pallas kernels: 20.9 us -> 20.6 us  [local(): pl.pallas_call(functools.partial(whole_kernel, sizes), out_shape=pltpu.VM...]
where the time goes in v3:
time: 21.4 us; the launch traced here: 21.3 us
  Pallas kernels  20.6 us (96%)
  local copies, waits for them, and re-layouts  0.64 us (3%)
    pallas_call x1, Pallas kernels, local(): pl.pallas_call(functools.partial(whole_kernel, sizes), out_shape=pltpu.VM...  20.6 us
    unnamed x1, local copies, waits for them, and re-layouts  0.64 us

profile of v3, /device:TPU:0, one launch (start us, length us, event | category | flops | bytes accessed | tf_op | source)
XLA Modules:
  0.0 21.3 jit_solution(13508042899453943540)
XLA Ops:
  0.0 20.6 %shard_map.55 = f32[8,24,128]{2,1,0:T(8,128)S(1)} custom-call(f32[2,4]{1,0:T(2,128)} %bitcast.9, f32[4]{0:T(128)} %height_h.1, f32[64,64,256]{2,1,0:T(8,128)} %bitcast.7, s32[1,4,16]{2,1,0:T(4,128)} %kept_h.1, s32[4,1,16]{2,1,0:T(1,128)} %bitcast.8), custom_call_target="tpu_custom_call" | custom-call | tf_op jit(solution)/shard_map/pallas_call | solution.py:529
  20.6 0.6 %copy.8 = f32[1,1,8,24,128]{4,3,2,1,0:T(8,128)} copy(f32[1,1,8,24,128]{4,3,2,1,0:T(8,128)S(1)} %bitcast.6) | data formatting | bytes 196608
